TPU v7x, 32 devices: a whole 2x2x4 slice. The times are simulated.
32 devices in a mesh: wide: 8 (over y, x, core), narrow: 4 (over z).
Axes of the slice: x: 2, y: 2, z: 4, core: 2. Of those that a mesh axis runs over, the one named last changes fastest.
Arguments:
- coefficients: float32 [8, 8192, 8192], P(None, 'wide', 'narrow'), may hold values from -0.07 to 0.07
- tensor_blocks: float32 [8, 32, 8192], P(None, 'wide', 'narrow'), may hold values from -6 to 6
- basis_rows: float32 [32, 8192], P(None, ('wide', 'narrow')), may hold values from -1.1 to 1.1, as said below
Outputs:
- new_basis: float32 [32, 8192], P(None, ('wide', 'narrow'))
- projection: float32 [32, 32], replicated
- factor: float32 [32, 32], replicated
Inputs may be any that keep to these rules, and one draw needn't show every extreme that they name: The rows of basis_rows are nearly but not exactly orthonormal: basis_rows basis_rows^T differs from the identity by less than 0.2 in spectral norm.
All inputs are finite; a program needn't handle non-finite values.
Results may differ from a plain program's by a relative error of at most 0.0002.
Values sent between devices are 32-bit elements; how exact they have to be, the bound alone decides.
A program may use at most 128 MiB of HBM per device.

v0:
```python
import functools

import jax
import jax.numpy as jnp
from jax import lax
from jax.experimental import pallas as pl
from jax.experimental.pallas import tpu as pltpu
from jax.sharding import PartitionSpec as P

MESH = pl.DeviceIdType.MESH
HI = lax.Precision.HIGHEST
F32 = jnp.float32
DEPTH = 4


def nt(a, b):
    return lax.dot_general(a, b, (((1,), (1,)), ((), ())), precision=HI, preferred_element_type=F32)


def nn(a, b):
    return lax.dot_general(a, b, (((1,), (0,)), ((), ())), precision=HI, preferred_element_type=F32)


def fold(x):
    return 128 // x.shape[1] if 128 % x.shape[1] == 0 and x.shape[0] % (128 // x.shape[1]) == 0 else 1


def pack(x, f):
    r = x.shape[0] // f
    return jnp.concatenate([x[q * r:(q + 1) * r] for q in range(f)], axis=1)


def unpack(x, f):
    c = x.shape[1] // f
    return jnp.concatenate([x[:, q * c:(q + 1) * c] for q in range(f)], axis=0)


def split(x):
    hi = x.astype(jnp.bfloat16)
    return hi, (x - hi.astype(F32)).astype(jnp.bfloat16)


def kernel(wide, narrow, total, coef, tens, basis, out_x, out_proj_t, out_gram,
           buf, tg, tf, ts, acc, bs, part, img, az1, aw1, az2, aw2,
           csem, lsem, t_send, t_recv, b_send, b_recv, r_send, r_recv,
           z1_send, z1_recv, w1_send, w1_recv, z2_send, z2_recv, w2_send, w2_recv):
    w = lax.axis_index("wide")
    n = lax.axis_index("narrow")
    terms, own, cols = tens.shape
    ranks = own * wide
    rows = basis.shape[1]
    half = wide // 2
    depth = min(DEPTH, terms)
    sib = w + 1 - 2 * lax.rem(w, 2)

    def peer(d):
        return lax.rem(w + 2 * d, wide)

    def sibpeer(d):
        return lax.rem(sib + 2 * d, wide)

    def zpeer(d):
        return lax.rem(n + d, narrow)

    def remote(src, dst, ss, rs, dev):
        return pltpu.make_async_remote_copy(
            src_ref=src, dst_ref=dst, send_sem=ss, recv_sem=rs, device_id=dev, device_id_type=MESH)

    def block(j):
        return lax.rem(n + 1 + j, narrow)

    def load(k, j):
        r0 = pl.multiple_of(block(j) * rows, rows)
        s = lax.rem(k, depth)
        return pltpu.make_async_copy(coef.at[k, pl.ds(r0, rows), :], buf.at[s, j], csem.at[s, j])

    local_t = pltpu.make_async_copy(tens, tg.at[:, w], lsem.at[0])
    local_b = pltpu.make_async_copy(basis, bs.at[n], lsem.at[1])
    local_t.start()
    local_b.start()
    for k in range(depth):
        for j in range(narrow):
            load(k, j).start()

    barrier = pltpu.get_barrier_semaphore()

    @pl.loop(1, wide)
    def _(d):
        pl.semaphore_signal(barrier, inc=1, device_id=(lax.rem(w + d, wide), n), device_id_type=MESH)

    for d in range(1, narrow):
        pl.semaphore_signal(barrier, inc=1, device_id=(w, zpeer(d)), device_id_type=MESH)
    pl.semaphore_wait(barrier, wide - 1 + narrow - 1)

    def t_out(k, d):
        return remote(tg.at[k, w], tg.at[k, w], t_send.at[k, d], t_recv.at[k, w], (peer(d), n))

    def t_sib(k):
        return remote(tg.at[k, w], tg.at[k, w], t_send.at[k, 0], t_recv.at[k, w], (sib, n))

    def t_fwd(k, d):
        p = peer(d)
        return remote(tg.at[k, p], tg.at[k, p], t_send.at[k, half + d], t_recv.at[k, p], (sib, n))

    def t_in(k, p):
        remote(tg.at[k, p], tg.at[k, p], t_send.at[k, 0], t_recv.at[k, p], (sib, n)).wait_recv()

    local_t.wait()

    @pl.loop(0, terms)
    def _(k):
        @pl.loop(1, half)
        def _(d):
            t_out(k, d).start()

        t_sib(k).start()

    local_b.wait()

    def b_out(d):
        return remote(bs.at[n], bs.at[n], b_send.at[d], b_recv.at[n], (w, zpeer(d)))

    for d in range(1, narrow):
        b_out(d).start()

    def forward(k):
        @pl.loop(1, half)
        def _(d):
            t_in(k, peer(d))
            t_fwd(k, d).start()

    def prepare(k):
        @pl.loop(0, half)
        def _(d):
            t_in(k, sibpeer(d))

        for q in range(wide):
            tf[q * own:(q + 1) * own, :] = tg[k, q]
        hi, lo = split(tf[...])
        ts[0:ranks, :] = hi
        ts[ranks:2 * ranks, :] = lo

    def product(s, j):
        hi, lo = split(buf[s, j])
        dims = (((1,), (1,)), ((), ()))
        t = ts[...]
        return (lax.dot_general(hi, t, dims, preferred_element_type=F32)
                + lax.dot_general(lo, t, dims, preferred_element_type=F32))

    acc[...] = jnp.zeros_like(acc)
    forward(0)

    @pl.loop(0, terms - 1)
    def _(k):
        s = lax.rem(k, depth)
        prepare(k)
        group = max(1, narrow // 2)
        for g in range(0, narrow, group):
            for j in range(g, g + group):
                load(k, j).wait()
            for j in range(g, g + group):
                acc[j] += product(s, j)
            for j in range(g, g + group):
                @pl.when(k + depth < terms)
                def _():
                    load(k + depth, j).start()
            if g == 0:
                forward(k + 1)

    last = terms - 1
    prepare(last)
    for d in range(1, narrow):
        q = zpeer(d)
        remote(bs.at[q], bs.at[q], b_send.at[d], b_recv.at[q], (w, q)).wait_recv()
    me = bs[n]
    corr = nt(me, me)

    def r_out(j):
        q = block(j)
        return remote(part.at[j], img.at[n], r_send.at[j], r_recv.at[n], (w, q))

    first_t = jnp.zeros((ranks, bs.shape[1]), F32)
    for j in range(narrow):
        load(last, j).wait()
        v = (acc[j] + product(last % depth, j)).T
        p = v[0:ranks] + v[ranks:2 * ranks]
        if j < narrow - 1:
            part[j] = p
            r_out(j).start()
        else:
            img[n] = p
        first_t = first_t + nt(p, bs[block(j)])

    def all_reduce(value, az, aw, zs, zr, ws, wr):
        f = fold(value)
        az[n] = pack(value, f)

        def z_out(d):
            return remote(az.at[n], az.at[n], zs.at[d], zr.at[n], (w, zpeer(d)))

        for d in range(1, narrow):
            z_out(d).start()
        for d in range(1, narrow):
            q = zpeer(d)
            remote(az.at[q], az.at[q], zs.at[d], zr.at[q], (w, q)).wait_recv()
        t = az[0]
        for q in range(1, narrow):
            t = t + az[q]
        aw[w] = t

        def w_out(d):
            return remote(aw.at[w], aw.at[w], ws.at[d], wr.at[w], (lax.rem(w + d, wide), n))

        for d in range(1, wide):
            w_out(d).start()
        for d in range(1, wide):
            q = lax.rem(w + d, wide)
            remote(aw.at[q], aw.at[q], ws.at[d], wr.at[q], (q, n)).wait_recv()
        t = aw[0]
        for q in range(1, wide):
            t = t + aw[q]

        def finish():
            for d in range(1, narrow):
                z_out(d).wait_send()
            for d in range(1, wide):
                w_out(d).wait_send()

        return unpack(t, f), finish

    m = bs.shape[1]
    both, finish1 = all_reduce(jnp.concatenate([first_t, corr], axis=0), az1, aw1,
                               z1_send, z1_recv, w1_send, w1_recv)
    first_t = both[0:ranks]
    corr = both[ranks:ranks + m]
    proj_t = first_t + (first_t - nn(first_t, corr))
    for d in range(1, narrow):
        q = zpeer(d)
        remote(img.at[q], img.at[q], r_send.at[0], r_recv.at[q], (w, q)).wait_recv()
    image = img[0]
    for q in range(1, narrow):
        image = image + img[q]
    x = image - nn(proj_t, me)
    gram, finish2 = all_reduce(nt(x, x), az2, aw2, z2_send, z2_recv, w2_send, w2_recv)
    out_x[...] = x
    out_proj_t[...] = proj_t
    out_gram[...] = gram * (1.0 / total)

    finish1()
    finish2()
    for j in range(narrow - 1):
        r_out(j).wait_send()
    for d in range(1, narrow):
        b_out(d).wait_send()

    @pl.loop(0, terms)
    def _(k):
        t_sib(k).wait_send()

        @pl.loop(1, half)
        def _(d):
            t_out(k, d).wait_send()
            t_fwd(k, d).wait_send()


def finish(x_in, proj_t, gram, out_new, out_proj, out_fac):
    a = gram[...]
    x = x_in[...]
    ranks = a.shape[0]
    sub = lax.broadcasted_iota(jnp.int32, (ranks, 1), 0)
    scale = jnp.ones((ranks, 1), F32)
    for j in range(ranks):
        rs = 1.0 / jnp.sqrt(a[j:j + 1, j:j + 1])
        lcol = jnp.where(sub > j, a[:, j:j + 1] * rs, 0.0)
        arow = a[j:j + 1, :] * rs
        xrow = x[j:j + 1, :] * rs
        scale = jnp.where(sub == j, rs, scale)
        a = a - lcol * arow
        x = x - lcol * xrow
    out_new[...] = x * scale
    upper = a * scale
    r_i = lax.broadcasted_iota(jnp.int32, (ranks, ranks), 0)
    c_i = lax.broadcasted_iota(jnp.int32, (ranks, ranks), 1)
    out_fac[...] = jnp.where(c_i >= r_i, upper, 0.0).T
    out_proj[...] = proj_t[...].T


def body(wide, narrow, total, coefficients, tensor_blocks, basis_rows):
    terms, own, cols = tensor_blocks.shape
    m, rows = basis_rows.shape
    ranks = own * wide
    depth = min(DEPTH, terms)
    def packed(r, c):
        f = fold(jax.ShapeDtypeStruct((r, c), F32))
        return (r // f, c * f)

    dma = lambda *s: pltpu.SemaphoreType.DMA(s)
    vm = lambda s, t=F32: pltpu.VMEM(s, t)
    x, proj_t, gram = pl.pallas_call(
        functools.partial(kernel, wide, narrow, total),
        out_shape=(
            jax.ShapeDtypeStruct((ranks, rows), F32),
            jax.ShapeDtypeStruct((ranks, m), F32),
            jax.ShapeDtypeStruct((ranks, ranks), F32),
        ),
        in_specs=[pl.BlockSpec(memory_space=pl.ANY)] * 3,
        out_specs=[pl.BlockSpec(memory_space=pltpu.VMEM)] * 3,
        scratch_shapes=[
            vm((depth, narrow, rows, cols)),
            vm((terms, wide, own, cols)),
            vm((ranks, cols)),
            vm((2 * ranks, cols), jnp.bfloat16),
            vm((narrow, rows, 2 * ranks)),
            vm((narrow, m, rows)),
            vm((narrow, ranks, rows)),
            vm((narrow, ranks, rows)),
            vm((narrow,) + packed(ranks + m, m)),
            vm((wide,) + packed(ranks + m, m)),
            vm((narrow,) + packed(ranks, ranks)),
            vm((wide,) + packed(ranks, ranks)),
            dma(depth, narrow), dma(2),
            dma(terms, wide), dma(terms, wide),
            dma(narrow), dma(narrow), dma(narrow), dma(narrow),
            dma(narrow), dma(narrow), dma(wide), dma(wide),
            dma(narrow), dma(narrow), dma(wide), dma(wide),
        ],
        compiler_params=pltpu.CompilerParams(
            collective_id=0, has_side_effects=True, vmem_limit_bytes=60 * 1024 * 1024),
        name="krylov_step",
    )(coefficients, tensor_blocks, basis_rows)
    return pl.pallas_call(
        finish,
        out_shape=(
            jax.ShapeDtypeStruct((ranks, rows), F32),
            jax.ShapeDtypeStruct((m, ranks), F32),
            jax.ShapeDtypeStruct((ranks, ranks), F32),
        ),
        in_specs=[pl.BlockSpec(memory_space=pltpu.VMEM)] * 3,
        out_specs=[pl.BlockSpec(memory_space=pltpu.VMEM)] * 3,
        name="krylov_finish",
    )(x, proj_t, gram)


def solution(mesh):
    wide, narrow = mesh.shape["wide"], mesh.shape["narrow"]
    in_specs = (P(None, "wide", "narrow"), P(None, "wide", "narrow"), P(None, ("wide", "narrow")))
    out_specs = (P(None, ("wide", "narrow")), P(), P())

    def whole(coefficients, tensor_blocks, basis_rows):
        total = coefficients.shape[1]
        return jax.shard_map(functools.partial(body, wide, narrow, total), mesh=mesh,
                             in_specs=in_specs, out_specs=out_specs, check_vma=False)(
            coefficients, tensor_blocks, basis_rows)

    return whole
```

profile of v0, /device:TPU:0, one launch (start us, length us, event | category | flops | bytes accessed | tf_op | source)
XLA Modules:
  0.0 62.0 jit_solution(14474374931164872829)
XLA Ops:
  0.6 56.7 %krylov_step.1 = (f32[32,256]{1,0:T(8,128)}, f32[32,32]{1,0:T(8,128)}, f32[32,32]{1,0:T(8,128)}) custom-call(f32[8,1024,2048]{2,1,0:T(8,128)} %coef.1, f32[8,4,2048]{2,1,0:T(4,128)} %tens.1, f32[32,256]{1,0:T(8,128)} %basis.1), custom_call_target="tpu_custom_call" | custom-call | tf_op jit(solution)/shard_map/krylov_step/pallas_call | solution.py:299
  57.3 4.7 %krylov_finish.1 = (f32[32,256]{1,0:T(8,128)}, f32[32,32]{1,0:T(8,128)}, f32[32,32]{1,0:T(8,128)}) custom-call(f32[32,256]{1,0:T(8,128)} %get-tuple-element.6.x_in, f32[32,32]{1,0:T(8,128)} %get-tuple-element.7.proj_t, f32[32,32]{1,0:T(8,128)} %get-tuple-element.8.gram), custom_call_target="tpu_custom_call" | custom-call | tf_op jit(solution)/shard_map/krylov_finish/pallas_call | solution.py:331
where the time goes:
time: 62.2 us; the launch traced here: 62 us
  Pallas kernels  61.4 us (99%)
  between operations  0.64 us (1%)
    pallas_call x1, Pallas kernels, body(): pl.pallas_call(functools.partial(kernel, wide, narrow, total), out_shape=...  56.7 us
    pallas_call x1, Pallas kernels, body(): pl.pallas_call(finish, out_shape=(jax.ShapeDtypeStruct((ranks, rows), F32...  4.68 us

commit v1 on v0

v1 whole, which is shorter than its diff:
```python
import functools

import jax
import jax.numpy as jnp
from jax import lax
from jax.experimental import pallas as pl
from jax.experimental.pallas import tpu as pltpu
from jax.sharding import PartitionSpec as P

MESH = pl.DeviceIdType.MESH
HI = lax.Precision.HIGHEST
F32 = jnp.float32
BF16 = jnp.bfloat16
DEPTH = 5
PANEL = 8
LANES = 128
TILE = 256
GROUP = 4
NT = (((1,), (1,)), ((), ()))
NN = (((1,), (0,)), ((), ()))


def nt(a, b):
    return lax.dot_general(a, b, NT, precision=HI, preferred_element_type=F32)


def nn(a, b):
    return lax.dot_general(a, b, NN, precision=HI, preferred_element_type=F32)


def fold(r, c):
    return 128 // c if 128 % c == 0 and r % (128 // c) == 0 else 1


def pack(x, f):
    r = x.shape[0] // f
    return jnp.concatenate([x[q * r:(q + 1) * r] for q in range(f)], axis=1)


def unpack(x, f):
    c = x.shape[1] // f
    return jnp.concatenate([x[:, q * c:(q + 1) * c] for q in range(f)], axis=0)


def packed(r, c):
    f = fold(r, c)
    return (r // f, c * f)


def split(x):
    hi = x.astype(BF16)
    return hi, (x - hi.astype(F32)).astype(BF16)


def each(lo, hi, f):
    if hi - lo <= 8:
        for d in range(lo, hi):
            f(d)
    else:
        pl.loop(lo, hi)(f)


def widen(x, width):
    return x[:, :width] if width <= LANES else jnp.concatenate([x] * (width // LANES), axis=1)


def factor_solve(a, x):
    ranks, rows = x.shape
    sub = lax.broadcasted_iota(jnp.int32, (ranks, LANES), 0)
    r_i = lax.broadcasted_iota(jnp.int32, (ranks, ranks), 0)
    c_i = lax.broadcasted_iota(jnp.int32, (ranks, ranks), 1)
    scale = jnp.ones((ranks, LANES), F32)
    lower = jnp.zeros((ranks, ranks), F32)
    panel = PANEL if ranks % PANEL == 0 else 1
    for b0 in range(0, ranks, panel):
        cols = [jnp.broadcast_to(a[:, b0 + t:b0 + t + 1], (ranks, LANES)) for t in range(panel)]
        for t in range(panel):
            j = b0 + t
            rs = lax.rsqrt(cols[t][j:j + 1, :])
            full = cols[t] * rs
            lower = jnp.where((c_i == j) & (r_i >= j), full[:, :ranks], lower)
            below = jnp.where(sub > j, full, 0.0)
            scale = jnp.where(sub == j, rs, scale)
            for u in range(t + 1, panel):
                cols[u] = cols[u] - below * below[b0 + u:b0 + u + 1, :]
            if j + 1 < ranks:
                a = a - below[:, :ranks] * (a[j:j + 1, :] * rs[:, :ranks])
                x = x - widen(below, rows) * (x[j:j + 1, :] * widen(rs, rows))
    return x * widen(scale, rows), lower


def kernel(wide, narrow, coef, tens, basis, out_image, out_sums, out_hm,
           buf, own_buf, tg, tf, ts, tt, acc, low, me_ref, part, img, sums, hm, azc, awc, azs, aws,
           csem, osem, lsem, xsem, t_send, t_recv, r_send, r_recv, c_sem, s_sem):
    w = lax.axis_index("wide")
    n = lax.axis_index("narrow")
    terms, own, cols = tens.shape
    ranks = own * wide
    m, rows = basis.shape
    half = wide // 2
    depth = min(DEPTH, terms)
    away = narrow - 1
    tile = TILE if cols % TILE == 0 else cols
    group = GROUP if terms % GROUP == 0 else 1
    sib = w + 1 - 2 * lax.rem(w, 2)

    def peer(d):
        return lax.rem(w + 2 * d, wide)

    def zpeer(d):
        return lax.rem(n + d, narrow)

    def remote(src, dst, ss, rs, dev):
        return pltpu.make_async_remote_copy(
            src_ref=src, dst_ref=dst, send_sem=ss, recv_sem=rs, device_id=dev, device_id_type=MESH)

    def block(j):
        return lax.rem(n + 1 + j, narrow)

    def source(k, j):
        r0 = pl.multiple_of(block(j) * rows, rows)
        return coef.at[k, pl.ds(r0, rows), :]

    def fetch(k):
        for j in range(away):
            pltpu.make_async_copy(source(k, j), buf.at[k % depth, j], csem.at[k % depth]).start()

    def load(k, lo, count):
        dst = buf.at[k % depth, pl.ds(lo, count)]
        return pltpu.make_async_copy(dst, dst, csem.at[k % depth])

    def fetch_own(k):
        pltpu.make_async_copy(source(k, away), own_buf.at[k], osem.at[k // group]).start()

    def load_own(g):
        dst = own_buf.at[pl.ds(g * group, group)]
        return pltpu.make_async_copy(dst, dst, osem.at[g])

    local_t = pltpu.make_async_copy(tens, tg.at[:, w], lsem.at[0])
    local_b = pltpu.make_async_copy(basis, me_ref, lsem.at[1])
    local_t.start()
    local_b.start()

    barrier = pltpu.get_barrier_semaphore()

    @pl.loop(1, wide)
    def _(d):
        pl.semaphore_signal(barrier, inc=1, device_id=(lax.rem(w + d, wide), n), device_id_type=MESH)

    for d in range(1, narrow):
        pl.semaphore_signal(barrier, inc=1, device_id=(w, zpeer(d)), device_id_type=MESH)
    local_t.wait()
    local_b.wait()
    for k in range(depth):
        fetch(k)
    me = me_ref[...]
    azc[n] = pack(nt(me, me), fold(m, m))
    pl.semaphore_wait(barrier, wide - 1 + narrow - 1)

    def t_out(k, d):
        return remote(tg.at[k, w], tg.at[k, w], t_send, t_recv.at[k, 0], (peer(d), n))

    def t_sib(k):
        return remote(tg.at[k, w], tg.at[k, w], t_send, t_recv.at[k, 1], (sib, n))

    def t_fwd(k, d):
        p = peer(d)
        return remote(tg.at[k, p], tg.at[k, p], t_send, t_recv.at[k, 1], (sib, n))

    def t_in(k, i, count):
        some = tg.at[k, pl.ds(0, count)]
        remote(some, some, t_send, t_recv.at[k, i], (sib, n)).wait_recv()

    @pl.loop(0, terms)
    def _(k):
        each(1, half, lambda d: t_out(k, d).start())
        t_sib(k).start()

    def forward(k):
        t_in(k, 0, half - 1)
        each(1, half, lambda d: t_fwd(k, d).start())

    def prepare(k):
        t_in(k, 1, half)
        for q in range(wide):
            tf[q * own:(q + 1) * own, :] = tg[k, q]
        hi, lo = split(tf[...])
        ts[k] = hi
        tt[k] = jnp.concatenate([hi, lo], axis=0).T

    def products(work):
        highs, lows = [None] * len(work), [None] * len(work)

        def stream(i, c):
            k, view = work[i]
            hi, _ = split(view[:, c:c + tile])
            p = lax.dot_general(hi, tt[k, c:c + tile, :], NN, preferred_element_type=F32)
            highs[i] = p if c == 0 else highs[i] + p

        def push(i, c):
            k, view = work[i]
            _, lo = split(view[:, c:c + tile])
            q = lax.dot_general(ts[k, :, c:c + tile], lo, NT, preferred_element_type=F32)
            lows[i] = q if c == 0 else lows[i] + q

        for c in range(0, cols, tile):
            for i in range(len(work)):
                push(i, c)
                stream(i, c)
        return highs, lows

    def reducer(az, aw, sems):
        def z_out(d):
            return remote(az.at[n], az.at[n], sems.at[0], sems.at[1], (w, zpeer(d)))

        def w_out(d):
            return remote(aw.at[w], aw.at[w], sems.at[2], sems.at[3], (lax.rem(w + d, wide), n))

        some_z = az.at[pl.ds(0, narrow - 1)]
        some_w = aw.at[pl.ds(0, wide - 1)]
        all_z = remote(some_z, some_z, sems.at[0], sems.at[1], (sib, n))
        all_w = remote(some_w, some_w, sems.at[2], sems.at[3], (sib, n))

        def z_start():
            for d in range(1, narrow):
                z_out(d).start()

        def z_finish():
            all_z.wait_recv()
            t = az[0]
            for q in range(1, narrow):
                t = t + az[q]
            aw[w] = t
            each(1, wide, lambda d: w_out(d).start())

        def w_finish():
            all_w.wait_recv()
            t = aw[0]
            for q in range(1, wide):
                t = t + aw[q]
            return t

        def drain():
            all_z.wait_send()
            all_w.wait_send()

        return z_start, z_finish, w_finish, drain

    c_start, c_mid, c_end, c_drain = reducer(azc, awc, c_sem)
    s_start, s_mid, s_end, s_drain = reducer(azs, aws, s_sem)
    c_start()
    forward(0)
    prepare(0)

    def advance(k, lo, hi):
        load(k, lo, hi - lo).wait()
        highs, lows = products([(k, buf.at[k % depth, j]) for j in range(lo, hi)])
        for j, p, q in zip(range(lo, hi), highs, lows):
            acc[j] = p if k == 0 else acc[j] + p
            low[j] = q if k == 0 else low[j] + q
        if k + depth < terms and hi == away:
            fetch(k + depth)

    for k in range(terms):
        if k == 0:
            advance(0, 0, away)
            if terms > 1:
                forward(1)
        else:
            prepare(k)
            advance(k, 0, away)
        if k + depth == terms:
            for q in range(terms):
                fetch_own(q)
        if k + 2 < terms:
            forward(k + 2)
        if k == 1:
            c_mid()

    def r_out(j):
        return remote(part.at[j], img.at[n], r_send, r_recv, (w, block(j)))

    some_img = img.at[pl.ds(0, away)]
    all_r = remote(part, some_img, r_send, r_recv, (sib, n))

    def settle(high, lows):
        v = high.T
        return v[0:ranks] + v[ranks:2 * ranks] + lows

    for j in range(away):
        part[j] = settle(acc[j], low[j])
        r_out(j).start()

    corr = unpack(c_end(), fold(m, m))
    eye = jnp.where(lax.broadcasted_iota(jnp.int32, (m, m), 0) == lax.broadcasted_iota(jnp.int32, (m, m), 1), 1.0, 0.0)
    e = corr - eye
    e2 = nn(e, e)
    hm[0] = eye - e
    hm[1] = (eye - e) + (e2 - nn(e, e2))
    put_hm = pltpu.make_async_copy(hm, out_hm, xsem.at[0])
    put_hm.start()

    high, lows = None, None
    for g in range(terms // group):
        load_own(g).wait()
        ps, qs = products([(k, own_buf.at[k]) for k in range(g * group, g * group + group)])
        p, q = functools.reduce(jnp.add, ps), functools.reduce(jnp.add, qs)
        high = p if g == 0 else high + p
        lows = q if g == 0 else lows + q

    image = settle(high, lows)
    all_r.wait_recv()
    for d in range(1, narrow):
        image = image + img[zpeer(d)]
    img[n] = image
    put_image = pltpu.make_async_copy(img.at[n], out_image, xsem.at[1])
    put_image.start()
    me = me_ref[...]
    both = nt(image, jnp.concatenate([me, image], axis=0))
    azs[n] = pack(both, fold(ranks, m + ranks))
    s_start()
    c_drain()
    all_r.wait_send()
    sent = tg.at[:, pl.ds(0, wide - 1)]
    remote(sent, sent, t_send, t_recv.at[0, 0], (sib, n)).wait_send()
    put_hm.wait()
    put_image.wait()
    s_mid()
    sums[...] = s_end()
    put_sums = pltpu.make_async_copy(sums, out_sums, xsem.at[2])
    put_sums.start()
    s_drain()
    put_sums.wait()


def finish(total, image_in, sums_in, hm_in, basis_in, new_out, proj_out, fac_out,
           image, sums, hm, me, new, proj, fac, sem):
    ins = [pltpu.make_async_copy(s, d, sem.at[i]) for i, (s, d) in enumerate(
        ((sums_in, sums), (hm_in, hm), (image_in, image), (basis_in, me)))]
    for c in ins:
        c.start()
    for c in ins:
        c.wait()
    m = me.shape[0]
    ranks = image.shape[0]
    both = unpack(sums[...], fold(ranks, m + ranks))
    first_t = both[:, 0:m]
    square = both[:, m:m + ranks]
    proj_t = nn(first_t, hm[0])
    gram = (square - nt(nn(first_t, hm[1]), first_t)) * (1.0 / total)
    proj[...] = nt(hm[0], first_t)
    x, lower = factor_solve(gram, image[...] - nn(proj_t, me[...]))
    new[...] = x
    fac[...] = lower
    outs = [pltpu.make_async_copy(s, d, sem.at[i]) for i, (s, d) in enumerate(
        ((new, new_out), (proj, proj_out), (fac, fac_out)))]
    for c in outs:
        c.start()
    for c in outs:
        c.wait()


def body(wide, narrow, total, coefficients, tensor_blocks, basis_rows):
    terms, own, cols = tensor_blocks.shape
    m, rows = basis_rows.shape
    ranks = own * wide
    depth = min(DEPTH, terms)
    dma = lambda *s: pltpu.SemaphoreType.DMA(s)
    vm = lambda s, t=F32: pltpu.VMEM(s, t)
    shape = lambda *s: jax.ShapeDtypeStruct(s, F32)
    anywhere = pl.BlockSpec(memory_space=pl.ANY)
    cpack, spack = packed(m, m), packed(ranks, m + ranks)
    image, sums, hm = pl.pallas_call(
        functools.partial(kernel, wide, narrow),
        out_shape=(shape(ranks, rows), shape(*spack), shape(2, m, m)),
        in_specs=[anywhere] * 3,
        out_specs=[anywhere] * 3,
        scratch_shapes=[
            vm((depth, narrow - 1, rows, cols)),
            vm((terms, rows, cols)),
            vm((terms, wide, own, cols)),
            vm((ranks, cols)),
            vm((terms, ranks, cols), BF16),
            vm((terms, cols, 2 * ranks), BF16),
            vm((narrow - 1, rows, 2 * ranks)),
            vm((narrow - 1, ranks, rows)),
            vm((m, rows)),
            vm((narrow - 1, ranks, rows)),
            vm((narrow, ranks, rows)),
            vm(spack),
            vm((2, m, m)),
            vm((narrow,) + cpack),
            vm((wide,) + cpack),
            vm((narrow,) + spack),
            vm((wide,) + spack),
            dma(depth), dma(terms), dma(2), dma(3),
            pltpu.SemaphoreType.DMA, dma(terms, 2),
            pltpu.SemaphoreType.DMA, pltpu.SemaphoreType.DMA, dma(4), dma(4),
        ],
        compiler_params=pltpu.CompilerParams(
            collective_id=0, has_side_effects=True, vmem_limit_bytes=62 * 1024 * 1024),
        name="krylov_step",
    )(coefficients, tensor_blocks, basis_rows)
    return pl.pallas_call(
        functools.partial(finish, total),
        out_shape=(shape(ranks, rows), shape(m, ranks), shape(ranks, ranks)),
        in_specs=[anywhere] * 4,
        out_specs=[anywhere] * 3,
        scratch_shapes=[
            vm((ranks, rows)), vm(spack), vm((2, m, m)), vm((m, rows)),
            vm((ranks, rows)), vm((m, ranks)), vm((ranks, ranks)), dma(4),
        ],
        name="krylov_finish",
    )(image, sums, hm, basis_rows)


def solution(mesh):
    wide, narrow = mesh.shape["wide"], mesh.shape["narrow"]
    in_specs = (P(None, "wide", "narrow"), P(None, "wide", "narrow"), P(None, ("wide", "narrow")))
    out_specs = (P(None, ("wide", "narrow")), P(), P())

    def whole(coefficients, tensor_blocks, basis_rows):
        total = coefficients.shape[1]
        return jax.shard_map(functools.partial(body, wide, narrow, total), mesh=mesh,
                             in_specs=in_specs, out_specs=out_specs, check_vma=False)(
            coefficients, tensor_blocks, basis_rows)

    return whole
```

time: 62.2 us -> 41.1 us (0.66)
  Pallas kernels: 61.4 us -> 40.1 us
    pallas_call x2, Pallas kernels: 61.4 us -> 40.1 us  [the longest x1 37.5 us: body(): pl.pallas_call(functools.partial(kernel, wide, narrow), out_shape=(shape(...]
where the time goes in v1:
time: 41.1 us; the launch traced here: 40.9 us
  Pallas kernels  40.1 us (98%)
  between operations  0.8 us (2%)
    pallas_call x1, Pallas kernels, body(): pl.pallas_call(functools.partial(kernel, wide, narrow), out_shape=(shape(...  37.5 us
    pallas_call x1, Pallas kernels, body(): pl.pallas_call(functools.partial(finish, total), out_shape=(shape(ranks,...  2.62 us

profile of v1, /device:TPU:0, one launch (start us, length us, event | category | flops | bytes accessed | tf_op | source)
XLA Modules:
  0.0 40.9 jit_solution(11718087462410046130)
XLA Ops:
  0.6 37.5 %krylov_step.1 = (f32[32,256]{1,0:T(8,128)}, f32[16,128]{1,0:T(8,128)}, f32[2,32,32]{2,1,0:T(8,128)}) custom-call(f32[8,1024,2048]{2,1,0:T(8,128)} %coef.1, f32[8,4,2048]{2,1,0:T(4,128)} %tens.1, f32[32,256]{1,0:T(8,128)} %basis_in.1), custom_call_target="tpu_custom_call" | custom-call | tf_op jit(solution)/shard_map/krylov_step/pallas_call | solution.py:373
  38.1 2.6 %krylov_finish.1 = (f32[32,256]{1,0:T(8,128)}, f32[32,32]{1,0:T(8,128)}, f32[32,32]{1,0:T(8,128)}) custom-call(f32[32,256]{1,0:T(8,128)} %get-tuple-element.6.image_in, f32[16,128]{1,0:T(8,128)} %get-tuple-element.7.sums_in, f32[2,32,32]{2,1,0:T(8,128)} %get-tuple-element.8.hm_in, f32[32,256]{1,0:T(8,128)} %basis_in.1), custom_call_target="tpu_custom_call" | custom-call | tf_op jit(solution)/shard_map/krylov_finish/pallas_call | solution.py:404

commit v2 on v1

--- a/solution.py
+++ b/solution.py
@@ -11,7 +11,7 @@
 HI = lax.Precision.HIGHEST
 F32 = jnp.float32
 BF16 = jnp.bfloat16
-DEPTH = 5
+DEPTH = 6
 PANEL = 8
 LANES = 128
 TILE = 256
@@ -90,8 +90,8 @@
 
 
 def kernel(wide, narrow, coef, tens, basis, out_image, out_sums, out_hm,
-           buf, own_buf, tg, tf, ts, tt, acc, low, me_ref, part, img, sums, hm, azc, awc, azs, aws,
-           csem, osem, lsem, xsem, t_send, t_recv, r_send, r_recv, c_sem, s_sem):
+           buf, tg, tf, ts, tt, acc, low, me_ref, part, img, azc, awc, azs, aws,
+           csem, osem, lsem, t_send, t_recv, r_send, r_recv, c_sem, s_sem):
     w = lax.axis_index("wide")
     n = lax.axis_index("narrow")
     terms, own, cols = tens.shape
@@ -125,16 +125,15 @@
         for j in range(away):
             pltpu.make_async_copy(source(k, j), buf.at[k % depth, j], csem.at[k % depth]).start()
 
-    def load(k, lo, count):
-        dst = buf.at[k % depth, pl.ds(lo, count)]
+    def load(k):
+        dst = buf.at[k % depth]
         return pltpu.make_async_copy(dst, dst, csem.at[k % depth])
 
-    def fetch_own(k):
-        pltpu.make_async_copy(source(k, away), own_buf.at[k], osem.at[k // group]).start()
-
-    def load_own(g):
-        dst = own_buf.at[pl.ds(g * group, group)]
-        return pltpu.make_async_copy(dst, dst, osem.at[g])
+    def own_view(k):
+        return buf.at[(terms - depth + k // away) % depth, k % away]
+
+    def load_own(k):
+        return pltpu.make_async_copy(source(k, away), own_view(k), osem.at[k])
 
     local_t = pltpu.make_async_copy(tens, tg.at[:, w], lsem.at[0])
     local_b = pltpu.make_async_copy(basis, me_ref, lsem.at[1])
@@ -253,7 +252,8 @@
     prepare(0)
 
     def advance(k, lo, hi):
-        load(k, lo, hi - lo).wait()
+        if lo == 0:
+            load(k).wait()
         highs, lows = products([(k, buf.at[k % depth, j]) for j in range(lo, hi)])
         for j, p, q in zip(range(lo, hi), highs, lows):
             acc[j] = p if k == 0 else acc[j] + p
@@ -261,18 +261,27 @@
         if k + depth < terms and hi == away:
             fetch(k + depth)
 
+    def halves(k):
+        advance(k, 0, 1)
+        if k + 1 < terms:
+            forward(k + 1)
+        if away > 1:
+            advance(k, 1, away)
+
     for k in range(terms):
         if k == 0:
-            advance(0, 0, away)
-            if terms > 1:
-                forward(1)
+            halves(0)
         else:
             prepare(k)
-            advance(k, 0, away)
-        if k + depth == terms:
-            for q in range(terms):
-                fetch_own(q)
-        if k + 2 < terms:
+            if k == 1:
+                halves(1)
+            else:
+                advance(k, 0, away)
+        if k + depth >= terms:
+            q = (k + depth - terms) * away
+            for i in range(q, min(q + away, terms)):
+                load_own(i).start()
+        if k and k + 2 < terms:
             forward(k + 2)
         if k == 1:
             c_mid()
@@ -295,15 +304,14 @@
     eye = jnp.where(lax.broadcasted_iota(jnp.int32, (m, m), 0) == lax.broadcasted_iota(jnp.int32, (m, m), 1), 1.0, 0.0)
     e = corr - eye
     e2 = nn(e, e)
-    hm[0] = eye - e
-    hm[1] = (eye - e) + (e2 - nn(e, e2))
-    put_hm = pltpu.make_async_copy(hm, out_hm, xsem.at[0])
-    put_hm.start()
+    out_hm[0] = eye - e
+    out_hm[1] = (eye - e) + (e2 - nn(e, e2))
 
     high, lows = None, None
     for g in range(terms // group):
-        load_own(g).wait()
-        ps, qs = products([(k, own_buf.at[k]) for k in range(g * group, g * group + group)])
+        for k in range(g * group, g * group + group):
+            load_own(k).wait()
+        ps, qs = products([(k, own_view(k)) for k in range(g * group, g * group + group)])
         p, q = functools.reduce(jnp.add, ps), functools.reduce(jnp.add, qs)
         high = p if g == 0 else high + p
         lows = q if g == 0 else lows + q
@@ -312,9 +320,7 @@
     all_r.wait_recv()
     for d in range(1, narrow):
         image = image + img[zpeer(d)]
-    img[n] = image
-    put_image = pltpu.make_async_copy(img.at[n], out_image, xsem.at[1])
-    put_image.start()
+    out_image[...] = image
     me = me_ref[...]
     both = nt(image, jnp.concatenate([me, image], axis=0))
     azs[n] = pack(both, fold(ranks, m + ranks))
@@ -323,24 +329,12 @@
     all_r.wait_send()
     sent = tg.at[:, pl.ds(0, wide - 1)]
     remote(sent, sent, t_send, t_recv.at[0, 0], (sib, n)).wait_send()
-    put_hm.wait()
-    put_image.wait()
     s_mid()
-    sums[...] = s_end()
-    put_sums = pltpu.make_async_copy(sums, out_sums, xsem.at[2])
-    put_sums.start()
+    out_sums[...] = s_end()
     s_drain()
-    put_sums.wait()
-
-
-def finish(total, image_in, sums_in, hm_in, basis_in, new_out, proj_out, fac_out,
-           image, sums, hm, me, new, proj, fac, sem):
-    ins = [pltpu.make_async_copy(s, d, sem.at[i]) for i, (s, d) in enumerate(
-        ((sums_in, sums), (hm_in, hm), (image_in, image), (basis_in, me)))]
-    for c in ins:
-        c.start()
-    for c in ins:
-        c.wait()
+
+
+def finish(total, image, sums, hm, me, new_out, proj_out, fac_out, new, proj, fac, sem):
     m = me.shape[0]
     ranks = image.shape[0]
     both = unpack(sums[...], fold(ranks, m + ranks))
@@ -369,15 +363,15 @@
     vm = lambda s, t=F32: pltpu.VMEM(s, t)
     shape = lambda *s: jax.ShapeDtypeStruct(s, F32)
     anywhere = pl.BlockSpec(memory_space=pl.ANY)
+    inside = pl.BlockSpec(memory_space=pltpu.VMEM)
     cpack, spack = packed(m, m), packed(ranks, m + ranks)
     image, sums, hm = pl.pallas_call(
         functools.partial(kernel, wide, narrow),
         out_shape=(shape(ranks, rows), shape(*spack), shape(2, m, m)),
-        in_specs=[anywhere] * 3,
-        out_specs=[anywhere] * 3,
+        in_specs=[pl.BlockSpec(memory_space=pltpu.HBM)] * 3,
+        out_specs=[inside] * 3,
         scratch_shapes=[
             vm((depth, narrow - 1, rows, cols)),
-            vm((terms, rows, cols)),
             vm((terms, wide, own, cols)),
             vm((ranks, cols)),
             vm((terms, ranks, cols), BF16),
@@ -387,29 +381,27 @@
             vm((m, rows)),
             vm((narrow - 1, ranks, rows)),
             vm((narrow, ranks, rows)),
-            vm(spack),
-            vm((2, m, m)),
             vm((narrow,) + cpack),
             vm((wide,) + cpack),
             vm((narrow,) + spack),
             vm((wide,) + spack),
-            dma(depth), dma(terms), dma(2), dma(3),
+            dma(depth), dma(terms), dma(2),
             pltpu.SemaphoreType.DMA, dma(terms, 2),
             pltpu.SemaphoreType.DMA, pltpu.SemaphoreType.DMA, dma(4), dma(4),
         ],
         compiler_params=pltpu.CompilerParams(
-            collective_id=0, has_side_effects=True, vmem_limit_bytes=62 * 1024 * 1024),
+            collective_id=0, has_side_effects=True, vmem_limit_bytes=48 * 1024 * 1024),
         name="krylov_step",
-    )(coefficients, tensor_blocks, basis_rows)
+    )(*[pltpu.with_memory_space_constraint(x, pltpu.HBM) for x in (coefficients, tensor_blocks, basis_rows)])
     return pl.pallas_call(
         functools.partial(finish, total),
         out_shape=(shape(ranks, rows), shape(m, ranks), shape(ranks, ranks)),
-        in_specs=[anywhere] * 4,
+        in_specs=[inside] * 4,
         out_specs=[anywhere] * 3,
         scratch_shapes=[
-            vm((ranks, rows)), vm(spack), vm((2, m, m)), vm((m, rows)),
-            vm((ranks, rows)), vm((m, ranks)), vm((ranks, ranks)), dma(4),
+            vm((ranks, rows)), vm((m, ranks)), vm((ranks, ranks)), dma(3),
         ],
+        compiler_params=pltpu.CompilerParams(vmem_limit_bytes=4 * 1024 * 1024),
         name="krylov_finish",
     )(image, sums, hm, basis_rows)
 

time: 41.1 us -> 39.5 us (0.961)
  Pallas kernels: 40.1 us -> 38.5 us
    pallas_call x1, Pallas kernels: 37.5 us -> 36.7 us  [body(): pl.pallas_call(functools.partial(kernel, wide, narrow), out_shape=(shape(...]
    pallas_call x1, Pallas kernels: 2.62 us -> 1.81 us  [body(): pl.pallas_call(functools.partial(finish, total), out_shape=(shape(ranks,...]
where the time goes in v2:
time: 39.5 us; the launch traced here: 39.3 us
  Pallas kernels  38.5 us (97%)
  between operations  0.81 us (2%)
    pallas_call x1, Pallas kernels, body(): pl.pallas_call(functools.partial(kernel, wide, narrow), out_shape=(shape(...  36.7 us
    pallas_call x1, Pallas kernels, body(): pl.pallas_call(functools.partial(finish, total), out_shape=(shape(ranks,...  1.81 us

profile of v2, /device:TPU:0, one launch (start us, length us, event | category | flops | bytes accessed | tf_op | source)
XLA Modules:
  0.0 39.3 jit_solution(17217728554177331212)
XLA Ops:
  0.6 0.0 copy-start
  0.6 36.7 %krylov_step.1 = (f32[32,256]{1,0:T(8,128)S(1)}, f32[16,128]{1,0:T(8,128)S(1)}, f32[2,32,32]{2,1,0:T(8,128)S(1)}) custom-call(f32[8,1024,2048]{2,1,0:T(8,128)} %coef.1, f32[8,4,2048]{2,1,0:T(4,128)} %tens.1, f32[32,256]{1,0:T(8,128)} %me.1), custom_call_target="tpu_custom_call" | custom-call | tf_op jit(solution)/shard_map/krylov_step/pallas_call | solution.py:368
  37.3 0.0 copy-done
  37.3 1.8 %krylov_finish.1 = (f32[32,256]{1,0:T(8,128)}, f32[32,32]{1,0:T(8,128)}, f32[32,32]{1,0:T(8,128)}) custom-call(f32[32,256]{1,0:T(8,128)S(1)} %get-tuple-element.6.image, f32[16,128]{1,0:T(8,128)S(1)} %get-tuple-element.7.sums, f32[2,32,32]{2,1,0:T(8,128)S(1)} %get-tuple-element.8.hm, f32[32,256]{1,0:T(8,128)S(1)} %copy-done), custom_call_target="tpu_custom_call" | custom-call | tf_op jit(solution)/shard_map/krylov_finish/pallas_call | solution.py:396
Async XLA Ops:
  0.6 36.7 %copy-start = (f32[32,256]{1,0:T(8,128)S(1)}, f32[32,256]{1,0:T(8,128)}, u32[]{:S(2)}) copy-start(f32[32,256]{1,0:T(8,128)} %me.1) | copy-start | bytes 98308
